TPU v7x, 32 devices: a whole 2x2x4 slice. The times are simulated.
32 devices in a mesh: ep: 4 (over y, core), fsdp: 8 (over z, x).
Axes of the slice: x: 2, y: 2, z: 4, core: 2. Of those that a mesh axis runs over, the one named last changes fastest.
Arguments:
- w_down: float32 [16, 6400, 4096], P('ep', None, 'fsdp'), may hold values from -0.109375 to 0.109375
- router_weight: float32 [4096, 16], P('fsdp', 'ep'), may hold values from -0.09375 to 0.09375
- router_gain: float32 [4096], P('fsdp'), may hold values from 0.25 to 1.75
Outputs:
- serve_down: bfloat16 [16, 6400, 4096], P('ep', 'fsdp')
- scale_down: float32 [16, 6400], P('ep', 'fsdp')
- serve_router: bfloat16 [4096, 16], replicated
All inputs are finite; a program needn't handle non-finite values.
Results may differ from a plain program's by a relative error of at most 0.001.
Values may be sent and summed in bfloat16 or wider, within the bound.
A program may use at most 192 MiB of HBM per device.

v0:
```python
import jax
import jax.numpy as jnp
from jax import lax
from jax.sharding import PartitionSpec as P


def body(w_down, router_weight, router_gain):
    total_down = lax.psum(jnp.sum(w_down * w_down, axis=2), "fsdp")
    scale_down = jnp.sqrt(total_down)
    narrow_down = (w_down / jnp.expand_dims(scale_down, 2)).astype(jnp.bfloat16)
    serve_down = lax.all_to_all(narrow_down, "fsdp", split_axis=1, concat_axis=2, tiled=True)
    scale_down = lax.dynamic_slice_in_dim(
        scale_down, lax.axis_index("fsdp") * serve_down.shape[1], serve_down.shape[1], axis=1
    )
    part_router = (router_weight * router_gain[:, None]).astype(jnp.bfloat16)
    row_router = lax.all_gather(part_router, "fsdp", axis=0, tiled=True)
    serve_router = lax.all_gather(row_router, "ep", axis=1, tiled=True)
    return (serve_down, scale_down, serve_router)


def solution(mesh):
    in_specs = (P("ep", None, "fsdp"), P("fsdp", "ep"), P("fsdp"))
    out_specs = (P("ep", "fsdp", None), P("ep", "fsdp"), P())
    return jax.shard_map(body, mesh=mesh, in_specs=in_specs, out_specs=out_specs, check_vma=False)
```

profile of v0, /device:TPU:0, one launch (start us, length us, event | category | flops | bytes accessed | tf_op | source)
XLA Modules:
  0.0 818.4 jit_solution(10136285089813340323)
XLA Ops:
  7.2 0.0 all-reduce.2.cloned.1.call-start
  7.2 17.4 %multiply_reduce_fusion = f32[4,6400]{1,0:T(4,128)} fusion(f32[4,6400,512]{2,1,0:T(8,128)} %param.3), kind=kLoop, calls=%fused_computation.1 | loop fusion | flops 26188800 | bytes 52531200 | tf_op jit(solution)/shard_map/reduce_sum | solution.py:8
  24.6 0.0 all-reduce.2.cloned.1.call-update
  24.6 72.5 %all-reduce.2.cloned.1.call-done = f32[4,6400]{1,0:T(4,128)} async-done(((f32[4,6400]{1,0:T(4,128)}), f32[4,6400]{1,0:T(4,128)}) %all-reduce.2.cloned.1.call-update) | async-done | bytes 102416 | tf_op jit(solution)/shard_map/psum | solution.py:8
  97.1 0.9 sqrt.3
  98.1 1.1 copy.7
  99.2 0.0 copy-start
  99.2 0.0 copy-start.1
  99.2 58.2 %fusion = bf16[4,6400,512]{2,0,1:T(4,128)(2,1)} fusion(f32[4,6400,512]{2,1,0:T(8,128)} %param.3, f32[4,6400]{0,1:T(8,128)S(1)} %copy.7), kind=kLoop, calls=%fused_computation.2 | loop fusion | flops 26214400 | bytes 78745600 | tf_op jit(solution)/shard_map/convert_element_type | solution.py:10
  157.4 6.5 all-to-all-start
  163.9 0.0 copy-done
  163.9 0.0 copy-done.1
  163.9 583.4 %all_gather.6 = bf16[4096,4]{0,1:T(4,128)(2,1)S(1)} all-gather(bf16[512,4]{0,1:T(4,128)(2,1)S(1)} %multiply_convert_fusion), channel_id=1, replica_groups=mesh['ep'=4,'fsdp'=8] {'fsdp'}, dimensions={0}, use_global_device_ids=true | all-gather | bytes 36864 | tf_op jit(solution)/shard_map/all_gather | solution.py:16
  747.3 5.4 all-gather
  752.8 0.7 reshape.9
  753.4 0.7 constant_dynamic-slice_fusion
  754.1 0.0 all-to-all-done
  754.1 18.2 %copy.9 = bf16[4,800,8,512]{3,2,1,0:T(8,128)(2,1)} copy(bf16[4,800,8,512]{3,0,1,2:T(4,128)(2,1)} %bitcast.1) | data formatting | bytes 52428800 | tf_op jit(solution)/shard_map/all_to_all | solution.py:11
  772.3 39.2 %all_to_all.16 = bf16[4,800,4096]{2,1,0:T(8,128)(2,1)} reshape(bf16[4,800,8,512]{3,2,1,0:T(8,128)(2,1)} %copy.9) | data formatting | bytes 52428800 | tf_op jit(solution)/shard_map/all_to_all | solution.py:11
  (1 shorter events, 0.0 us)
Async XLA Ops:
  7.2 90.0 %all-reduce.2.cloned.1.call-start = ((), (), s32[]{:S(2)}) async-start(), calls=%async_computation.1 | async-start | bytes 204800 | tf_op jit(solution)/shard_map/psum | solution.py:8
  99.2 64.7 %copy-start = (f32[512,4]{0,1:T(4,128)S(1)}, f32[512,4]{0,1:T(4,128)}, u32[]{:S(2)}) copy-start(f32[512,4]{0,1:T(4,128)} %param.4) | copy-start | bytes 24580
  99.2 64.7 %copy-start.1 = (f32[512]{0:T(512)S(1)}, f32[512]{0:T(512)}, u32[]{:S(2)}) copy-start(f32[512]{0:T(512)} %param.5) | copy-start | bytes 6148
  157.4 596.7 %all-to-all-start = ((bf16[4,6400,512]{2,0,1:T(4,128)(2,1)}), bf16[4,6400,512]{2,0,1:T(4,128)(2,1)}, u32[]{:S(2)}, u32[]{:S(2)}) async-start(bf16[4,6400,512]{2,0,1:T(4,128)(2,1)} %fusion), calls=%async_computation | async-start | bytes 52428800 | tf_op jit(solution)/shard_map/all_to_all | solution.py:11
Sparse Core Ops, SparseCore 0:
  24.8 72.3 all-reduce.1
where the time goes:
time: 820 us; the launch traced here: 818 us
  blocking collectives  589 us (72%)
  other arithmetic  75.6 us (9%)
  waiting for transfers between devices  72.5 us (9%)
  local copies, waits for them, and re-layouts  60.8 us (7%)
  between operations  14.1 us (2%)
    all_gather x1, blocking collectives, body(): row_router = lax.all_gather(part_router, 'fsdp', axis=0, tiled=True)  583 us
    psum x1, waiting for transfers between devices, body(): total_down = lax.psum(jnp.sum(w_down * w_down, axis=2), 'fsdp')  72.5 us
    convert_element_type x1, other arithmetic, body(): narrow_down = (w_down / jnp.expand_dims(scale_down, 2)).astype(jnp.bfloat16)  58.2 us
    all_to_all x2, local copies, waits for them, and re-layouts, body(): lax.all_to_all(narrow_down, 'fsdp', split_axis=1, concat_axis=2, tiled=True)  57.4 us
    reduce_sum x1, other arithmetic, body(): total_down = lax.psum(jnp.sum(w_down * w_down, axis=2), 'fsdp')  17.4 us
  transfers between devices with their start and end apart: 2, of which 1 were waited for; matrix products, arithmetic and copies ran while one was open for 0% of the time, Pallas kernels for 0%

commit v1 on v0

--- a/solution.py
+++ b/solution.py
@@ -5,7 +5,9 @@
 
 
 def body(w_down, router_weight, router_gain):
-    total_down = lax.psum(jnp.sum(w_down * w_down, axis=2), "fsdp")
+    x = jnp.sum(w_down * w_down, axis=2)
+    shards = lax.all_gather(x, "fsdp")
+    total_down = jnp.sum(shards, axis=0)
     scale_down = jnp.sqrt(total_down)
     narrow_down = (w_down / jnp.expand_dims(scale_down, 2)).astype(jnp.bfloat16)
     serve_down = lax.all_to_all(narrow_down, "fsdp", split_axis=1, concat_axis=2, tiled=True)

time: 820 us -> 763 us (0.930)
  waiting for transfers between devices: 72.5 us -> 0.01 us
  blocking collectives: 589 us -> 620 us
  between operations: 14.1 us -> 0.71 us
    psum x1 -> x0, waiting for transfers between devices: 72.5 us -> none  [body(): total_down = lax.psum(jnp.sum(w_down * w_down, axis=2), 'fsdp')]
    all_gather x0 -> x1, blocking collectives: none -> 33.9 us  [body(): shards = lax.all_gather(x, 'fsdp')]
    reduce_sum x1 -> x2, other arithmetic: 17.4 us -> 16.9 us  [the longest x1 16.8 us: body(): x = jnp.sum(w_down * w_down, axis=2)]
  transfers between devices with their start and end apart: 2 -> 1, of which waited for: 1 -> 0; matrix products, arithmetic and copies ran while one was open for 0% -> 0% of each run, Pallas kernels for 0% -> 0%
where the time goes in v1:
time: 763 us; the launch traced here: 762 us
  blocking collectives  620 us (81%)
  other arithmetic  74.8 us (10%)
  local copies, waits for them, and re-layouts  59.9 us (8%)
    all_gather x1, blocking collectives, body(): row_router = lax.all_gather(part_router, 'fsdp', axis=0, tiled=True)  580 us
    convert_element_type x1, other arithmetic, body(): narrow_down = (w_down / jnp.expand_dims(scale_down, 2)).astype(jnp.bfloat16)  57.9 us
    all_to_all x2, local copies, waits for them, and re-layouts, body(): lax.all_to_all(narrow_down, 'fsdp', split_axis=1, concat_axis=2, tiled=True)  57.4 us
    all_gather x1, blocking collectives, body(): shards = lax.all_gather(x, 'fsdp')  33.9 us
    reduce_sum x1, other arithmetic, body(): x = jnp.sum(w_down * w_down, axis=2)  16.8 us
  transfers between devices with their start and end apart: 1, of which 0 were waited for; matrix products, arithmetic and copies ran while one was open for 0% of the time, Pallas kernels for 0%

profile of v1, /device:TPU:0, one launch (start us, length us, event | category | flops | bytes accessed | tf_op | source)
XLA Modules:
  0.0 761.5 jit_solution(15995414812339284025)
XLA Ops:
  0.6 16.8 %multiply_reduce_fusion = f32[4,6400]{1,0:T(4,128)S(1)} fusion(f32[4,6400,512]{2,1,0:T(8,128)} %param.3), kind=kLoop, calls=%fused_computation.1 | loop fusion | flops 26188800 | bytes 52531200 | tf_op jit(solution)/shard_map/reduce_sum | solution.py:8
  17.4 33.9 %all-gather.1 = f32[8,4,6400]{2,1,0:T(4,128)S(1)} all-gather(f32[1,4,6400]{2,1,0:T(4,128)S(1)} %bitcast.10), channel_id=2, replica_groups=mesh['ep'=4,'fsdp'=8] {'fsdp'}, dimensions={0}, use_global_device_ids=true | all-gather | bytes 921600 | tf_op jit(solution)/shard_map/all_gather | solution.py:9
  51.3 0.1 reduce_sum.19
  51.5 0.1 sqrt.7
  51.5 1.1 copy.7
  52.6 0.0 copy-start
  52.7 0.0 copy-start.1
  52.7 57.9 %fusion = bf16[4,6400,512]{2,0,1:T(4,128)(2,1)} fusion(f32[4,6400,512]{2,1,0:T(8,128)} %param.3, f32[4,6400]{0,1:T(8,128)S(1)} %copy.7), kind=kLoop, calls=%fused_computation.2 | loop fusion | flops 26214400 | bytes 78745600 | tf_op jit(solution)/shard_map/convert_element_type | solution.py:12
  110.6 6.5 all-to-all-start
  117.1 0.0 copy-done
  117.1 0.0 copy-done.1
  117.1 580.2 %all_gather.14 = bf16[4096,4]{0,1:T(4,128)(2,1)S(1)} all-gather(bf16[512,4]{0,1:T(4,128)(2,1)S(1)} %multiply_convert_fusion), channel_id=1, replica_groups=mesh['ep'=4,'fsdp'=8] {'fsdp'}, dimensions={0}, use_global_device_ids=true | all-gather | bytes 36864 | tf_op jit(solution)/shard_map/all_gather | solution.py:18
  697.4 5.4 all-gather.2
  702.8 0.7 reshape.14
  703.5 0.7 constant_dynamic-slice_fusion
  704.1 0.0 all-to-all-done
  704.1 18.2 %copy.9 = bf16[4,800,8,512]{3,2,1,0:T(8,128)(2,1)} copy(bf16[4,800,8,512]{3,0,1,2:T(4,128)(2,1)} %bitcast.2) | data formatting | bytes 52428800 | tf_op jit(solution)/shard_map/all_to_all | solution.py:13
  722.4 39.2 %all_to_all.16 = bf16[4,800,4096]{2,1,0:T(8,128)(2,1)} reshape(bf16[4,800,8,512]{3,2,1,0:T(8,128)(2,1)} %copy.9) | data formatting | bytes 52428800 | tf_op jit(solution)/shard_map/all_to_all | solution.py:13
  (1 shorter events, 0.0 us)
Async XLA Ops:
  52.6 64.4 %copy-start = (f32[512,4]{0,1:T(4,128)S(1)}, f32[512,4]{0,1:T(4,128)}, u32[]{:S(2)}) copy-start(f32[512,4]{0,1:T(4,128)} %param.4) | copy-start | bytes 24580
  52.7 64.4 %copy-start.1 = (f32[512]{0:T(512)S(1)}, f32[512]{0:T(512)}, u32[]{:S(2)}) copy-start(f32[512]{0:T(512)} %param.5) | copy-start | bytes 6148
  110.6 593.6 %all-to-all-start = ((bf16[4,6400,512]{2,0,1:T(4,128)(2,1)}), bf16[4,6400,512]{2,0,1:T(4,128)(2,1)}, u32[]{:S(2)}, u32[]{:S(2)}) async-start(bf16[4,6400,512]{2,0,1:T(4,128)(2,1)} %fusion), calls=%async_computation | async-start | bytes 52428800 | tf_op jit(solution)/shard_map/all_to_all | solution.py:13

commit v2 on v0

--- a/solution.py
+++ b/solution.py
@@ -8,7 +8,9 @@
     total_down = lax.psum(jnp.sum(w_down * w_down, axis=2), "fsdp")
     scale_down = jnp.sqrt(total_down)
     narrow_down = (w_down / jnp.expand_dims(scale_down, 2)).astype(jnp.bfloat16)
-    serve_down = lax.all_to_all(narrow_down, "fsdp", split_axis=1, concat_axis=2, tiled=True)
+    pieces = jnp.split(narrow_down, lax.axis_size("fsdp"), axis=1)
+    received = lax.all_to_all(jnp.stack(pieces), "fsdp", 0, 0)
+    serve_down = jnp.concatenate(received, axis=2)
     scale_down = lax.dynamic_slice_in_dim(
         scale_down, lax.axis_index("fsdp") * serve_down.shape[1], serve_down.shape[1], axis=1
     )

time: 820 us -> 777 us (0.948)
  other arithmetic: 75.6 us -> 43.5 us
  local copies, waits for them, and re-layouts: 60.8 us -> 50.8 us
    all_to_all x2 -> x0, local copies, waits for them, and re-layouts: 57.4 us -> none  [body(): lax.all_to_all(narrow_down, 'fsdp', split_axis=1, concat_axis=2, tiled=True)]
    convert_element_type x1, other arithmetic: 58.2 us -> 26.1 us  [body(): narrow_down = (w_down / jnp.expand_dims(scale_down, 2)).astype(jnp.bfloat16)]
    unnamed x5 -> x12, local copies, waits for them, and re-layouts: 0.7 us -> 27.5 us
    reshape x0 -> x1, local copies, waits for them, and re-layouts: none -> 17.9 us  [body(): serve_down = jnp.concatenate(received, axis=2)]
where the time goes in v2:
time: 777 us; the launch traced here: 776 us
  blocking collectives  589 us (76%)
  waiting for transfers between devices  72.5 us (9%)
  local copies, waits for them, and re-layouts  50.8 us (7%)
  other arithmetic  43.5 us (6%)
  between operations  14.1 us (2%)
    all_gather x1, blocking collectives, body(): row_router = lax.all_gather(part_router, 'fsdp', axis=0, tiled=True)  583 us
    psum x1, waiting for transfers between devices, body(): total_down = lax.psum(jnp.sum(w_down * w_down, axis=2), 'fsdp')  72.5 us
    unnamed x12, local copies, waits for them, and re-layouts  27.5 us
    convert_element_type x1, other arithmetic, body(): narrow_down = (w_down / jnp.expand_dims(scale_down, 2)).astype(jnp.bfloat16)  26.1 us
    reshape x1, local copies, waits for them, and re-layouts, body(): serve_down = jnp.concatenate(received, axis=2)  17.9 us
    reduce_sum x1, other arithmetic, body(): total_down = lax.psum(jnp.sum(w_down * w_down, axis=2), 'fsdp')  17.4 us
  transfers between devices with their start and end apart: 2, of which 1 were waited for; matrix products, arithmetic and copies ran while one was open for 0% of the time, Pallas kernels for 0%

profile of v2, /device:TPU:0, one launch (start us, length us, event | category | flops | bytes accessed | tf_op | source)
XLA Modules:
  0.0 776.4 jit_solution(16197063411485344824)
XLA Ops:
  7.2 0.0 all-reduce.2.cloned.1.call-start
  7.2 17.4 %multiply_reduce_fusion = f32[4,6400]{1,0:T(4,128)} fusion(f32[4,6400,512]{2,1,0:T(8,128)} %param.3), kind=kLoop, calls=%fused_computation.1 | loop fusion | flops 26188800 | bytes 52531200 | tf_op jit(solution)/shard_map/reduce_sum | solution.py:8
  24.6 0.0 all-reduce.2.cloned.1.call-update
  24.6 72.5 %all-reduce.2.cloned.1.call-done = f32[4,6400]{1,0:T(4,128)} async-done(((f32[4,6400]{1,0:T(4,128)}), f32[4,6400]{1,0:T(4,128)}) %all-reduce.2.cloned.1.call-update) | async-done | bytes 102416 | tf_op jit(solution)/shard_map/psum | solution.py:8
  97.1 0.9 sqrt.3
  98.1 26.1 %divide_convert_fusion = bf16[4,6400,512]{2,1,0:T(8,128)(2,1)} fusion(f32[4,6400,512]{2,1,0:T(8,128)} %param.3, f32[4,6400]{1,0:T(4,128)S(1)} %sqrt.3), kind=kLoop, calls=%fused_computation | loop fusion | flops 26214400 | bytes 78745600 | tf_op jit(solution)/shard_map/convert_element_type | solution.py:10
  124.2 3.8 fusion.7
  128.0 3.8 fusion.6
  131.9 3.8 fusion.5
  135.7 3.8 fusion.4
  139.5 3.9 fusion.3
  143.4 3.8 fusion.2
  147.2 3.8 fusion.1
  151.0 3.8 fusion
  154.8 0.0 copy-start
  154.8 0.0 copy-start.1
  154.8 6.6 all-to-all-start
  161.4 0.0 copy-done
  161.5 0.0 copy-done.1
  161.5 583.4 %all_gather.6 = bf16[4096,4]{0,1:T(4,128)(2,1)S(1)} all-gather(bf16[512,4]{0,1:T(4,128)(2,1)S(1)} %multiply_convert_fusion), channel_id=1, replica_groups=mesh['ep'=4,'fsdp'=8] {'fsdp'}, dimensions={0}, use_global_device_ids=true | all-gather | bytes 36864 | tf_op jit(solution)/shard_map/all_gather | solution.py:18
  744.9 5.4 all-gather
  750.3 0.7 reshape.17
  751.0 0.7 constant_dynamic-slice_fusion
  751.7 0.0 all-to-all-done
  751.7 17.9 %copy.8 = bf16[8,4,100,8,512]{4,3,0,2,1:T(8,128)(2,1)} copy(bf16[8,4,100,8,512]{4,3,2,1,0:T(8,128)(2,1)} %bitcast.13) | data formatting | bytes 52428800 | tf_op jit(solution)/shard_map/reshape | solution.py:13
  (1 shorter events, 0.0 us)
Async XLA Ops:
  7.2 90.0 %all-reduce.2.cloned.1.call-start = ((), (), s32[]{:S(2)}) async-start(), calls=%async_computation.1 | async-start | bytes 204800 | tf_op jit(solution)/shard_map/psum | solution.py:8
  154.8 6.6 copy-start
  154.8 6.6 copy-start.1
  154.8 596.9 %all-to-all-start = ((bf16[8,4,800,512]{3,2,1,0:T(8,128)(2,1)}), bf16[8,4,800,512]{3,2,1,0:T(8,128)(2,1)}, u32[]{:S(2)}, u32[]{:S(2)}) async-start(bf16[8,4,800,512]{3,2,1,0:T(8,128)(2,1)} %fusion), calls=%async_computation | async-start | bytes 52428800 | tf_op jit(solution)/shard_map/all_to_all | solution.py:12
Sparse Core Ops, SparseCore 0:
  24.8 72.3 all-reduce.1
